TPU v7x, 32 devices: a whole 2x2x4 slice. The times are simulated.
32 devices in a mesh: vocab: 16 (over z, y, x), batch: 2 (over core).
Axes of the slice: x: 2, y: 2, z: 4, core: 2. Of those that a mesh axis runs over, the one named last changes fastest.
Arguments:
- hidden: bfloat16 [2048, 7168], P(('batch', 'vocab')), parts along dimension 0, may hold values from -1000 to 1000
- norm_gain: bfloat16 [7168], replicated, may hold values from 1.5 to 5
- lm_head: bfloat16 [7168, 16384], P(None, 'vocab'), may hold values from -2 to 2
- draft_logits: bfloat16 [2048, 16384], P('batch', 'vocab'), parts along dimension 0, may hold values from -480 to 480
- draft_tokens: int32 [2048], P('batch'), parts along dimension 0, may hold values from 0 to 16383
- tree_parents: int32 [2048], P('batch'), parts along dimension 0, may hold values from 0 to 62, as said below
- node_depths: int32 [2048], P('batch'), parts along dimension 0, may hold values from 0 to 8, as said below
- uniforms: float32 [2048], P('batch'), parts along dimension 0, may hold values from 0 to 1
Outputs:
- target_lse: float32 [2048], P('batch'), parts along dimension 0
- token_logprob: float32 [2048], P('batch'), parts along dimension 0
- residual_mass: float32 [2048], P('batch'), parts along dimension 0
- accept_margin: float32 [2048], P('batch'), parts along dimension 0
- path_margin: float32 [2048], P('batch'), parts along dimension 0
There are 2 independent parts, one for each index of `batch`. A program takes and returns all parts, laid end to end along the dimension named above; an argument that names none is the same for every part. Nothing has to cross between parts.
Inputs may be any that keep to these rules, and one draw needn't show every extreme that they name: `tree_parents`: rows come in 16 requests of 64 consecutive rows, the first of each being the root. A node's entry is the position of its parent within the request, smaller than its own position; the root's entry is 0. `node_depths`: A node's depth is its parent's depth plus one, the root's is 0; in every request some node has depth 8.
All inputs are finite; a program needn't handle non-finite values.
Results may differ from a plain program's by a relative error of at most 0.0049.
Values may be sent and summed in bfloat16 or wider, within the bound.
A program may use at most 128 MiB of HBM per device.

v0:
```python
import jax
import jax.numpy as jnp
from jax import lax
from jax.sharding import PartitionSpec as P

NODES = 64
DEPTH_MAX = 8


epsilon = 1e-06
highest = lax.Precision.HIGHEST


def merged(value, axis, join):
    pieces = jax.tree.map(lambda part: lax.all_gather(part, axis), value)
    head = jax.tree.map(lambda part: part[0], pieces)
    tail = jax.tree.map(lambda part: part[1:], pieces)
    total, _ = lax.scan(lambda total, share: (join(total, share), None), head, tail)
    return total


def normalize(hidden_rows, gain_vector):
    values = hidden_rows.astype(jnp.float32)
    mean_square = jnp.mean(values * values, axis=1, keepdims=True)
    scaled = values * lax.rsqrt(mean_square + epsilon) * gain_vector.astype(jnp.float32)
    return scaled.astype(jnp.bfloat16)


def join_stats(left_part, right_part):
    target_max = jnp.maximum(left_part[0], right_part[0])
    target_sum = left_part[1] * jnp.exp(left_part[0] - target_max) + right_part[1] * jnp.exp(
        right_part[0] - target_max
    )
    draft_max = jnp.maximum(left_part[2], right_part[2])
    draft_sum = left_part[3] * jnp.exp(left_part[2] - draft_max) + right_part[3] * jnp.exp(
        right_part[2] - draft_max
    )
    return (target_max, target_sum, draft_max, draft_sum)


def body(
    hidden, norm_gain, lm_head, draft_logits, draft_tokens, tree_parents, node_depths, uniforms
):
    vocab_dev = lm_head.shape[1]
    rows_all = draft_tokens.shape[0]
    requests = rows_all // NODES
    offset = lax.axis_index("vocab") * vocab_dev
    normed = normalize(hidden, norm_gain)
    local_column = draft_tokens - offset
    owned_here = (local_column >= 0) & (local_column < vocab_dev)
    vocab_iota = jnp.arange(vocab_dev, dtype=jnp.int32)
    column_hot = (local_column[:, None] == vocab_iota[None, :]) & owned_here[:, None]
    column_float = column_hot.astype(jnp.float32)
    column_half = column_hot.astype(jnp.bfloat16)
    node_iota = jnp.arange(NODES, dtype=jnp.int32)
    parent_hot = (
        tree_parents.reshape(requests, NODES)[:, :, None] == node_iota[None, None, :]
    ).astype(jnp.float32)

    def at_parent(vector):
        return jnp.einsum(
            "rkn,rn->rk", parent_hot, vector.reshape(requests, NODES), precision=highest
        ).reshape(rows_all)

    logits = jnp.dot(
        lax.all_gather(normed, "vocab", axis=0, tiled=True),
        lm_head,
        preferred_element_type=jnp.float32,
    )
    draft_values = draft_logits.astype(jnp.float32)
    local_target = jnp.max(logits, axis=1)
    local_draft = jnp.max(draft_values, axis=1)
    local_terms = (
        local_target,
        jnp.sum(jnp.exp(logits - local_target[:, None]), axis=1),
        local_draft,
        jnp.sum(jnp.exp(draft_values - local_draft[:, None]), axis=1),
    )
    target_max, target_sum, draft_max, draft_sum = merged(local_terms, "vocab", join_stats)
    target_lse = target_max + jnp.log(target_sum)
    draft_lse = draft_max + jnp.log(draft_sum)
    excess = jnp.maximum(
        jnp.exp(logits - target_lse[:, None]) - jnp.exp(draft_values - draft_lse[:, None]), 0.0
    )
    target_cols = jnp.einsum(
        "rnv,rkv->rnk",
        logits.reshape(requests, NODES, vocab_dev),
        column_float.reshape(requests, NODES, vocab_dev),
        precision=highest,
    )
    draft_cols = jnp.einsum(
        "rnv,rkv->rnk",
        draft_logits.reshape(requests, NODES, vocab_dev),
        column_half.reshape(requests, NODES, vocab_dev),
        preferred_element_type=jnp.float32,
    )
    picked_target = jnp.einsum("rkn,rnk->rk", parent_hot, target_cols).reshape(rows_all)
    picked_draft = jnp.einsum("rkn,rnk->rk", parent_hot, draft_cols).reshape(rows_all)
    picked_target, picked_draft = (picked_target, picked_draft)
    residual, picked_target, picked_draft = lax.psum(
        (jnp.sum(excess, axis=1), picked_target, picked_draft), "vocab"
    )
    target_lse, draft_lse, residual_mass, picked_target, picked_draft = (
        target_lse,
        draft_lse,
        residual,
        picked_target,
        picked_draft,
    )
    token_logprob = picked_target - at_parent(target_lse)
    draft_logprob = picked_draft - at_parent(draft_lse)
    accept_margin = jnp.exp(jnp.minimum(token_logprob - draft_logprob, 0.0)) - uniforms
    path_margin = jnp.ones((rows_all,), jnp.float32)
    for level_now in range(1, DEPTH_MAX + 1):
        path_margin = jnp.where(
            node_depths == level_now,
            jnp.minimum(accept_margin, at_parent(path_margin)),
            path_margin,
        )
    return (target_lse, token_logprob, residual_mass, accept_margin, path_margin)


def solution(mesh):
    return jax.shard_map(
        body,
        mesh=mesh,
        in_specs=(
            P(("batch", "vocab"), None),
            P(),
            P(None, "vocab"),
            P("batch", "vocab"),
            P("batch"),
            P("batch"),
            P("batch"),
            P("batch"),
        ),
        out_specs=(P("batch"), P("batch"), P("batch"), P("batch"), P("batch")),
        check_vma=False,
    )
```

profile of v0, /device:TPU:0, one launch (start us, length us, event | category | flops | bytes accessed | tf_op | source)
XLA Modules:
  0.0 383.4 jit_solution(11474094762704683032)
XLA Ops:
  7.2 0.9 convert_element_type.16
  8.1 1.5 fusion.15
  9.6 2.4 fusion.17
  12.0 0.4 reduce_max.28
  12.4 0.9 fusion.1
  13.3 43.9 %all-gather.3 = f32[16384]{0:T(1024)S(1)} all-gather(f32[1024]{0:T(1024)S(1)} %fusion.1), channel_id=5, replica_groups=mesh['vocab'=16,'batch'=2] {'vocab'}, dimensions={0}, use_global_device_ids=true | all-gather | bytes 69632 | tf_op jit(solution)/shard_map/all_gather | solution.py:15
  57.2 37.5 %all-gather.2 = f32[16384]{0:T(1024)S(1)} all-gather(f32[1024]{0:T(1024)S(1)} %reduce_max.32), channel_id=4, replica_groups=mesh['vocab'=16,'batch'=2] {'vocab'}, dimensions={0}, use_global_device_ids=true | all-gather | bytes 69632 | tf_op jit(solution)/shard_map/all_gather | solution.py:15
  94.9 0.2 fusion.43
  95.1 0.2 copy.17
  95.5 1.4 fusion.30
  97.0 0.6 fusion.40
  97.6 90.1 %all-gather.6.cloned.1.call-done = bf16[1024,7168]{1,0:T(8,128)(2,1)} async-done(((bf16[64,7168]{1,0:T(8,128)(2,1)}), bf16[1024,7168]{1,0:T(8,128)(2,1)}) %all-gather.6.cloned.1.call-update) | async-done | bytes 14680080 | tf_op jit(solution)/shard_map/all_gather | solution.py:66
  187.7 19.6 %fusion.54 = (f32[1024]{0:T(1024)S(1)}, f32[1024,1024]{1,0:T(8,128)S(1)}) fusion(bf16[1024,7168]{1,0:T(8,128)(2,1)} %all-gather.6.cloned.1.call-done, bf16[7168,1024]{1,0:T(8,128)(2,1)} %param.12), kind=kOutput, calls=%fused_computation.69 | convolution fusion | flops 15033433088 | bytes 33558528 | tf_op jit(solution)/shard_map/dot_general | solution.py:65
  207.4 1.9 copy-done
  209.3 1.1 exponential_reduce_fusion
  210.3 38.1 %all-gather.1 = f32[16384]{0:T(1024)S(1)} all-gather(f32[1024]{0:T(1024)S(1)} %exponential_reduce_fusion), channel_id=3, replica_groups=mesh['vocab'=16,'batch'=2] {'vocab'}, dimensions={0}, use_global_device_ids=true | all-gather | bytes 69632 | tf_op jit(solution)/shard_map/all_gather | solution.py:15
  248.4 36.0 %all-gather = f32[16384]{0:T(1024)S(1)} all-gather(f32[1024]{0:T(1024)S(1)} %get-tuple-element.91), channel_id=2, replica_groups=mesh['vocab'=16,'batch'=2] {'vocab'}, dimensions={0}, use_global_device_ids=true | all-gather | bytes 69632 | tf_op jit(solution)/shard_map/all_gather | solution.py:15
  284.5 1.8 while.16
  286.4 3.6 fusion.5
  290.1 5.0 %fusion.27 = f32[16,64]{1,0:T(8,128)S(1)} fusion(f32[16,64,64]{1,2,0:T(8,128)S(1)} %copy.17, f32[16,64,1024]{2,1,0:T(8,128)} %bitcast.67, s32[16,64]{1,0:T(8,128)S(1)} %eq.83, pred[16,64]{1,0:T(8,128)(4,1)S(1)} %and.16), kind=kOutput, calls=%fused_computation.31 | convolution fusion | flops 807533568 | bytes 4465664 | tf_op jit(solution)/shard_map/rnv,rkv->rnk/dot_general | solution.py:85
  295.2 0.6 fusion.42
  295.9 0.6 fusion.41
  296.5 73.6 %all-reduce = (f32[1024]{0:T(1024)S(1)}, f32[1024]{0:T(1024)}, f32[1024]{0:T(1024)S(1)}) all-reduce(f32[1024]{0:T(1024)S(1)} %reshape.125, f32[1024]{0:T(1024)S(1)} %fusion.5, f32[1024]{0:T(1024)S(1)} %reshape.129), channel_id=1, replica_groups=mesh['vocab'=16,'batch'=2] {'vocab'}, use_global_device_ids=true, to_apply=%region_7.8 | all-reduce | flops 3072 | bytes 24576 | tf_op jit(solution)/shard_map/psum | solution.py:100
  370.1 0.6 minimum_select_fusion.7
  370.8 0.6 fusion.39
  371.5 0.6 fusion.38
  372.3 0.6 fusion.37
  373.0 0.6 fusion.36
  373.8 0.6 fusion.35
  374.5 0.6 fusion.34
  375.3 0.6 fusion.33
  375.9 0.6 minimum_select_fusion
  (145 shorter events, 3.0 us)
Async XLA Ops:
  7.2 4.8 %copy-start.1 = (bf16[1024,1024]{1,0:T(8,128)(2,1)S(1)}, bf16[1024,1024]{1,0:T(8,128)(2,1)}, u32[]{:S(2)}) copy-start(bf16[1024,1024]{1,0:T(8,128)(2,1)} %param.13) | copy-start | bytes 6291460
  7.2 180.5 %all-gather.6.cloned.1.call-start = ((), (), s32[]{:S(2)}) async-start(), calls=%async_computation | async-start | bytes 15597568 | tf_op jit(solution)/shard_map/all_gather | solution.py:66
  8.1 86.7 %copy-start.7 = (s32[1024]{0:T(1024)S(1)}, s32[1024]{0:T(1024)}, u32[]{:S(2)}) copy-start(s32[1024]{0:T(1024)} %param.15) | copy-start | bytes 12292
  9.6 85.7 %copy-start.9 = (s32[1024]{0:T(1024)S(1)}, s32[1024]{0:T(1024)}, u32[]{:S(2)}) copy-start(s32[1024]{0:T(1024)} %param.14) | copy-start | bytes 12292
  57.2 150.1 %copy-start.4 = (f32[16384]{0:T(1024)}, f32[16384]{0:T(1024)S(1)}, u32[]{:S(2)}) copy-start(f32[16384]{0:T(1024)S(1)} %all-gather.3) | copy-start | bytes 196612
  94.7 112.6 %copy-start.5 = (f32[16384]{0:T(1024)}, f32[16384]{0:T(1024)S(1)}, u32[]{:S(2)}) copy-start(f32[16384]{0:T(1024)S(1)} %all-gather.2) | copy-start | bytes 196612
  207.3 1.9 copy-start
  207.3 77.1 %slice-start = ((f32[16384]{0:T(1024)}), f32[1024]{0:T(1024)S(1)}, s32[]{:S(2)}) async-start(f32[16384]{0:T(1024)} %copy-done.4), calls=%async_computation.1 | async-start | bytes 8192 | tf_op jit(solution)/shard_map/slice | solution.py:16
  207.4 77.1 %slice-start.1 = ((f32[16384]{0:T(1024)}), f32[1024]{0:T(1024)S(1)}, s32[]{:S(2)}) async-start(f32[16384]{0:T(1024)} %copy-done.5), calls=%async_computation.2 | async-start | bytes 8192 | tf_op jit(solution)/shard_map/slice | solution.py:16
  286.3 8.8 %copy-start.6 = (f32[1024]{0:T(1024)}, f32[1024]{0:T(1024)S(1)}, u32[]{:S(2)}) copy-start(f32[1024]{0:T(1024)S(1)} %get-tuple-element.94) | copy-start | bytes 12292
  290.0 80.1 %copy-start.2 = (s32[1024]{0:T(1024)S(1)}, s32[1024]{0:T(1024)}, u32[]{:S(2)}) copy-start(s32[1024]{0:T(1024)} %param.16) | copy-start | bytes 12292
  290.0 80.1 %copy-start.8 = (f32[1024]{0:T(1024)S(1)}, f32[1024]{0:T(1024)}, u32[]{:S(2)}) copy-start(f32[1024]{0:T(1024)} %param.17) | copy-start | bytes 12292
  370.7 5.8 %copy-start.3 = (f32[1024]{0:T(1024)}, f32[1024]{0:T(1024)S(1)}, u32[]{:S(2)}) copy-start(f32[1024]{0:T(1024)S(1)} %get-tuple-element.85) | copy-start | bytes 12292
Sparse Core Ops, SparseCore 0:
  12.1 175.5 all-gather.5
where the time goes:
time: 384 us; the launch traced here: 383 us
  blocking collectives  229 us (60%)
  waiting for transfers between devices  90.1 us (23%)
  matrix products  31.9 us (8%)
  between operations  14.3 us (4%)
  other arithmetic  12.4 us (3%)
  local copies, waits for them, and re-layouts  4.75 us (1%)
    all_gather x4, blocking collectives, merged(): pieces = jax.tree.map(lambda part: lax.all_gather(part, axis), value)  156 us
    all_gather x1, waiting for transfers between devices, body(): lax.all_gather(normed, 'vocab', axis=0, tiled=True)  90.1 us
    psum x1, blocking collectives, body(): lax.psum((jnp.sum(excess, axis=1), picked_target, picked_draft), 'vocab')  73.6 us
    dot_general x1, matrix products, body(): jnp.dot(lax.all_gather(normed, 'vocab', axis=0, tiled=True), lm_head, pre...  19.6 us
  transfers between devices with their start and end apart: 1, of which 1 were waited for; matrix products, arithmetic and copies ran while one was open for 1% of the time, Pallas kernels for 0%

commit v1 on v0

v1 whole, which is shorter than its diff:
```python
import functools

import jax
import jax.numpy as jnp
from jax import lax
from jax.experimental import pallas as pl
from jax.experimental.pallas import tpu as pltpu
from jax.sharding import PartitionSpec as P

NODES = 64
DEPTH_MAX = 8
MESH = pl.DeviceIdType.MESH
CHUNK_ROWS = 256
COLUMN_TILE = 256


epsilon = 1e-06
highest = lax.Precision.HIGHEST


def normalize(hidden_rows, gain_vector):
    values = hidden_rows.astype(jnp.float32)
    mean_square = jnp.mean(values * values, axis=1, keepdims=True)
    scaled = values * lax.rsqrt(mean_square + epsilon) * gain_vector.astype(jnp.float32)
    return scaled.astype(jnp.bfloat16)


def place_of(device, cycle, n):
    if n != 16:
        return device
    z, y, x = device // 4, (device // 2) % 2, device % 2
    corner = 2 * y + (x + y) % 2
    step = (corner + z) % 4
    return 4 * (z if cycle == 0 else corner) + step


def device_at(place, cycle, n):
    if n != 16:
        return place
    major = place // 4
    minor = (place % 4 + 4 - major) % 4
    z, corner = (major, minor) if cycle == 0 else (minor, major)
    y = corner // 2
    x = (corner + y) % 2
    return 4 * z + 2 * y + x


def gather_dot_kernel(
    n, parts, own_ref, head_ref, out_ref, held, head, own_sem, head_sem, send_sem, recv_sem
):
    streams, rows, width = own_ref.shape
    group = max(1, min(n, CHUNK_ROWS // rows))
    chunks = n // group
    columns = out_ref.shape[2]
    me = lax.axis_index("vocab")
    places = [place_of(me, cycle, n) for cycle in range(2)]

    def stream_kind(q):
        lane = q // parts
        return lane // 2, lane % 2

    def partner(q, steps):
        cycle, backward = stream_kind(q)
        hop = (n - steps) if backward else steps
        return device_at(lax.rem(places[cycle] + hop, n), cycle, n)

    own_copy = pltpu.make_async_copy(own_ref, held.at[0], own_sem)
    own_copy.start()
    head_copy = pltpu.make_async_copy(head_ref, head, head_sem)
    head_copy.start()

    ways = [partner(q, 1) for q in range(0, streams, parts)]
    barrier = pltpu.get_barrier_semaphore()
    for target in ways:
        pl.semaphore_signal(barrier, inc=1, device_id={"vocab": target}, device_id_type=MESH)
    pl.semaphore_wait(barrier, len(ways))

    def copy_of(q, step):
        return pltpu.make_async_remote_copy(
            src_ref=held.at[step, q],
            dst_ref=held.at[step + 1, q],
            send_sem=send_sem.at[step, q],
            recv_sem=recv_sem.at[step, q],
            device_id={"vocab": ways[q // parts]},
            device_id_type=MESH,
        )

    def multiply(chunk, q):
        first = chunk * group

        def tile(index, _):
            at = pl.multiple_of(index * COLUMN_TILE, COLUMN_TILE)
            block = jnp.concatenate([held[first + g, q] for g in range(group)], axis=0)
            part = jnp.dot(
                block, head[q, :, pl.ds(at, COLUMN_TILE)], preferred_element_type=jnp.float32
            )
            for g in range(group):
                cycle, backward = stream_kind(q)
                slot = first + g
                place = places[cycle] + slot if backward else places[cycle] + n - slot
                owner = device_at(lax.rem(place, n), cycle, n)
                piece = part[g * rows : (g + 1) * rows]
                out_ref[owner, :, pl.ds(at, COLUMN_TILE)] += piece
            return 0

        lax.fori_loop(0, columns // COLUMN_TILE, tile, 0)

    own_copy.wait()
    for q in range(streams):
        copy_of(q, 0).start()
    head_copy.wait()
    out_ref[...] = jnp.zeros_like(out_ref)

    return me, group, chunks, copy_of, multiply


def gather_dot_body(n, parts, *refs):
    streams = refs[0].shape[0]
    _, group, chunks, copy_of, multiply = gather_dot_kernel(n, parts, *refs)
    per_step = streams // group if group <= streams else 1
    spread = streams // per_step

    def run(chunk, turn):
        for k in range(per_step):
            q = turn * per_step + k
            if q < streams:
                multiply(chunk, q)

    def move(step):
        for q in range(streams):
            copy_of(q, step - 1).wait_recv()
            copy_of(q, step).start()

    def chunk_loop(chunk, _):
        for g in range(group):
            move(chunk * group + g)
            if g < spread:
                run(chunk - 1, g)
        return 0

    for step in range(1, group):
        move(step)
    lax.fori_loop(1, chunks - 1, chunk_loop, 0)
    for g in range(group):
        step = (chunks - 1) * group + g
        if step < n - 1:
            move(step)
        else:
            for q in range(streams):
                copy_of(q, step - 1).wait_recv()
        if g < spread:
            run(chunks - 2, g)
    for q in range(streams):
        multiply(chunks - 1, q)

    def drain(step, _):
        for q in range(streams):
            copy_of(q, step).wait_send()
        return 0

    lax.fori_loop(0, n - 1, drain, 0)


def gather_dot(normed, lm_head, n):
    rows, depth = normed.shape
    parts = 2 if n <= 16 else 1
    streams = 4 * parts
    width = depth // streams
    columns = lm_head.shape[1]
    own = normed.reshape(rows, streams, width).transpose(1, 0, 2)
    out = pl.pallas_call(
        functools.partial(gather_dot_body, n, parts),
        out_shape=jax.ShapeDtypeStruct((n, rows, columns), jnp.float32),
        in_specs=[pl.BlockSpec(memory_space=pl.ANY)] * 2,
        out_specs=pl.BlockSpec(memory_space=pltpu.VMEM),
        scratch_shapes=[
            pltpu.VMEM((n, streams, rows, width), jnp.bfloat16),
            pltpu.VMEM((streams, width, columns), jnp.bfloat16),
            pltpu.SemaphoreType.DMA,
            pltpu.SemaphoreType.DMA,
            pltpu.SemaphoreType.DMA((n - 1, streams)),
            pltpu.SemaphoreType.DMA((n - 1, streams)),
        ],
        compiler_params=pltpu.CompilerParams(
            collective_id=0, has_side_effects=True, vmem_limit_bytes=56 * 1024 * 1024
        ),
        name="gather_dot",
    )(own, lm_head.reshape(streams, width, columns))
    return out.reshape(n * rows, columns)


def exchange_kernel(n, x_ref, out_ref, own_sem, send_sem, recv_sem):
    me = lax.axis_index("vocab")
    barrier = pltpu.get_barrier_semaphore()

    def copy_to(d):
        return pltpu.make_async_remote_copy(
            src_ref=x_ref,
            dst_ref=out_ref.at[me],
            send_sem=send_sem.at[d],
            recv_sem=recv_sem.at[d],
            device_id={"vocab": lax.rem(me + d, n)},
            device_id_type=MESH,
        )

    def copy_from(d):
        return pltpu.make_async_remote_copy(
            src_ref=x_ref,
            dst_ref=out_ref.at[lax.rem(me + n - d, n)],
            send_sem=send_sem.at[d],
            recv_sem=recv_sem.at[d],
            device_id={"vocab": lax.rem(me + d, n)},
            device_id_type=MESH,
        )

    def greet(d, _):
        pl.semaphore_signal(
            barrier, inc=1, device_id={"vocab": lax.rem(me + d, n)}, device_id_type=MESH
        )
        return 0

    def send(d, _):
        copy_to(d).start()
        return 0

    def finish(d, _):
        copy_from(d).wait_recv()
        copy_to(d).wait_send()
        return 0

    own_copy = pltpu.make_async_copy(x_ref, out_ref.at[me], own_sem)
    own_copy.start()
    lax.fori_loop(1, n, greet, 0)
    pl.semaphore_wait(barrier, n - 1)
    lax.fori_loop(1, n, send, 0)
    lax.fori_loop(1, n, finish, 0)
    own_copy.wait()


def exchange(vectors, n, number):
    length = vectors[0].shape[0]
    packed = jnp.concatenate(vectors).reshape(-1, 128)
    out = pl.pallas_call(
        functools.partial(exchange_kernel, n),
        out_shape=jax.ShapeDtypeStruct((n,) + packed.shape, jnp.float32),
        in_specs=[pl.BlockSpec(memory_space=pltpu.VMEM)],
        out_specs=pl.BlockSpec(memory_space=pltpu.VMEM),
        scratch_shapes=[
            pltpu.SemaphoreType.DMA,
            pltpu.SemaphoreType.DMA((n,)),
            pltpu.SemaphoreType.DMA((n,)),
        ],
        compiler_params=pltpu.CompilerParams(collective_id=number, has_side_effects=True),
        name="exchange",
    )(packed)
    return out.reshape(n, len(vectors), length // 128, 128)


def body(
    n, hidden, norm_gain, lm_head, draft_logits, draft_tokens, tree_parents, node_depths, uniforms
):
    vocab_dev = lm_head.shape[1]
    rows_all = draft_tokens.shape[0]
    requests = rows_all // NODES
    offset = lax.axis_index("vocab") * vocab_dev
    normed = normalize(hidden, norm_gain)
    local_column = draft_tokens - offset
    owned_here = (local_column >= 0) & (local_column < vocab_dev)
    vocab_iota = jnp.arange(vocab_dev, dtype=jnp.int32)
    column_hot = (local_column[:, None] == vocab_iota[None, :]) & owned_here[:, None]
    column_float = column_hot.astype(jnp.float32)
    column_half = column_hot.astype(jnp.bfloat16)
    node_iota = jnp.arange(NODES, dtype=jnp.int32)
    parent_hot = (
        tree_parents.reshape(requests, NODES)[:, :, None] == node_iota[None, None, :]
    ).astype(jnp.float32)

    def at_parent(vector):
        return jnp.einsum(
            "rkn,rn->rk", parent_hot, vector.reshape(requests, NODES), precision=highest
        ).reshape(rows_all)

    logits = gather_dot(normed, lm_head, n)
    draft_values = draft_logits.astype(jnp.float32)
    local_target = jnp.max(logits, axis=1)
    local_draft = jnp.max(draft_values, axis=1)
    stats = exchange(
        (
            local_target,
            jnp.sum(jnp.exp(logits - local_target[:, None]), axis=1),
            local_draft,
            jnp.sum(jnp.exp(draft_values - local_draft[:, None]), axis=1),
        ),
        n,
        1,
    )

    def joined(maxima, sums):
        top = jnp.max(maxima, axis=0)
        total = jnp.sum(sums * jnp.exp(maxima - top), axis=0)
        return (top + jnp.log(total)).reshape(rows_all)

    target_lse = joined(stats[:, 0], stats[:, 1])
    draft_lse = joined(stats[:, 2], stats[:, 3])
    excess = jnp.maximum(
        jnp.exp(logits - target_lse[:, None]) - jnp.exp(draft_values - draft_lse[:, None]), 0.0
    )
    target_cols = jnp.einsum(
        "rnv,rkv->rnk",
        logits.reshape(requests, NODES, vocab_dev),
        column_float.reshape(requests, NODES, vocab_dev),
        precision=highest,
    )
    draft_cols = jnp.einsum(
        "rnv,rkv->rnk",
        draft_logits.reshape(requests, NODES, vocab_dev),
        column_half.reshape(requests, NODES, vocab_dev),
        preferred_element_type=jnp.float32,
    )
    picked_target = jnp.sum(parent_hot * target_cols.transpose(0, 2, 1), axis=2).reshape(rows_all)
    picked_draft = jnp.sum(parent_hot * draft_cols.transpose(0, 2, 1), axis=2).reshape(rows_all)
    shares = exchange((jnp.sum(excess, axis=1), picked_target, picked_draft), n, 2)
    sums = jnp.sum(shares, axis=0).reshape(3, rows_all)
    residual_mass, picked_target, picked_draft = sums[0], sums[1], sums[2]
    token_logprob = picked_target - at_parent(target_lse)
    draft_logprob = picked_draft - at_parent(draft_lse)
    accept_margin = jnp.exp(jnp.minimum(token_logprob - draft_logprob, 0.0)) - uniforms
    path_margin = jnp.ones((rows_all,), jnp.float32)
    for level_now in range(1, DEPTH_MAX + 1):
        path_margin = jnp.where(
            node_depths == level_now,
            jnp.minimum(accept_margin, at_parent(path_margin)),
            path_margin,
        )
    return (target_lse, token_logprob, residual_mass, accept_margin, path_margin)


def solution(mesh):
    return jax.shard_map(
        functools.partial(body, mesh.shape["vocab"]),
        mesh=mesh,
        in_specs=(
            P(("batch", "vocab"), None),
            P(),
            P(None, "vocab"),
            P("batch", "vocab"),
            P("batch"),
            P("batch"),
            P("batch"),
            P("batch"),
        ),
        out_specs=(P("batch"), P("batch"), P("batch"), P("batch"), P("batch")),
        check_vma=False,
    )
```

time: 384 us -> 227 us (0.59)
  blocking collectives: 229 us -> 0 us
  Pallas kernels: 0 us -> 193 us
  waiting for transfers between devices: 90.1 us -> 0 us
  matrix products: 31.9 us -> 10.1 us
  between operations: 14.3 us -> 0.81 us
  other arithmetic: 12.4 us -> 19.3 us
    pallas_call x0 -> x3, Pallas kernels: none -> 193 us  [the longest x1 172 us: gather_dot(): pl.pallas_call(functools.partial(gather_dot_body, n, parts), out_shape=ja...]
    all_gather x4 -> x0, blocking collectives: 156 us -> none  [merged(): pieces = jax.tree.map(lambda part: lax.all_gather(part, axis), value)]
    all_gather x1 -> x0, waiting for transfers between devices: 90.1 us -> none  [body(): lax.all_gather(normed, 'vocab', axis=0, tiled=True)]
    psum x1 -> x0, blocking collectives: 73.6 us -> none  [body(): lax.psum((jnp.sum(excess, axis=1), picked_target, picked_draft), 'vocab')]
    dot_general x1 -> x0, matrix products: 19.6 us -> none  [body(): jnp.dot(lax.all_gather(normed, 'vocab', axis=0, tiled=True), lm_head, pre...]
  transfers between devices with their start and end apart: 1 -> 0, of which waited for: 1 -> 0; matrix products, arithmetic and copies ran while one was open for 1% -> 0% of each run, Pallas kernels for 0% -> 0%
where the time goes in v1:
time: 227 us
  Pallas kernels  193 us (85%)
  other arithmetic  19.3 us (9%)
  matrix products  10.1 us (4%)
  local copies, waits for them, and re-layouts  3.57 us (2%)
    pallas_call x1, Pallas kernels, gather_dot(): pl.pallas_call(functools.partial(gather_dot_body, n, parts), out_shape=ja...  172 us
    pallas_call x2, Pallas kernels, exchange(): pl.pallas_call(functools.partial(exchange_kernel, n), out_shape=jax.Shape...  21.4 us
    dot_general x1, matrix products, body(): jnp.einsum('rnv,rkv->rnk', logits.reshape(requests, NODES, vocab_dev), co...  5.01 us

profile of v1, /device:TPU:0, one launch (start us, length us, event | category | flops | bytes accessed | tf_op | source)
XLA Modules:
  0.0 226.8 jit_solution(2303943014841098365)
XLA Ops:
  0.6 0.7 convert_element_type.16
  1.3 1.5 fusion.16
  2.8 1.5 fusion.18
  4.3 1.1 copy.42
  5.4 171.5 %gather_dot.1 = f32[16,64,1024]{2,1,0:T(8,128)} custom-call(bf16[8,64,896]{2,1,0:T(8,128)(2,1)} %bitcast.117, bf16[8,896,1024]{2,1,0:T(8,128)(2,1)} %bitcast.115), custom_call_target="tpu_custom_call" | custom-call | tf_op jit(solution)/shard_map/gather_dot/pallas_call | solution.py:171
  176.9 2.6 %reduce_max.45 = f32[16,64]{1,0:T(8,128)S(1)} reduce(f32[16,64,1024]{2,1,0:T(8,128)} %gather_dot.1, f32[]{:T(128)} %constant.6.clone.1), dimensions={2}, to_apply=%region_1.0 | reduce | flops 1047552 | bytes 4198404 | tf_op jit(solution)/shard_map/reduce_max | solution.py:285
  179.5 2.9 %exponential_reduce_fusion = f32[16,64]{1,0:T(8,128)S(1)} fusion(f32[16,64,1024]{2,1,0:T(8,128)} %gather_dot.1, f32[16,64]{1,0:T(8,128)S(1)} %reduce_max.45), kind=kLoop, calls=%fused_computation.11 | loop fusion | flops 2096128 | bytes 4202496 | tf_op jit(solution)/shard_map/reduce_sum | solution.py:290
  182.6 0.3 reduce_max.46
  183.0 0.9 fusion.1
  183.9 0.6 pad_maximum_fusion.x_ref
  184.5 10.1 %exchange.2 = f32[16,32,128]{2,1,0:T(8,128)} custom-call(f32[32,128]{1,0:T(8,128)} %pad_maximum_fusion.x_ref), custom_call_target="tpu_custom_call" | custom-call | tf_op jit(solution)/shard_map/exchange/pallas_call | solution.py:243
  194.6 0.9 bitcast_reduce_fusion
  195.5 1.0 fusion.52
  196.5 3.6 %fusion.5 = f32[1024]{0:T(1024)S(1)} fusion(bf16[1024,1024]{1,0:T(8,128)(2,1)S(1)} %copy-done, f32[16,64,1024]{2,1,0:T(8,128)} %gather_dot.1, f32[1024]{0:T(1024)S(1)} %bitcast.122, f32[1024]{0:T(1024)S(1)} %bitcast.120), kind=kLoop, calls=%fused_computation.7 | loop fusion | flops 6290432 | bytes 6303744 | tf_op jit(solution)/shard_map/reduce_sum | solution.py:322
  200.4 5.0 %fusion.25 = f32[16,64]{1,0:T(8,128)S(1)} fusion(f32[16,64,1024]{2,1,0:T(8,128)} %gather_dot.1, s32[16,64]{1,0:T(8,128)S(1)} %eq.83, pred[16,64]{1,0:T(8,128)(4,1)S(1)} %and.16, s32[16,64]{1,0:T(8,128)S(1)} %eq.79), kind=kOutput, calls=%fused_computation.26 | convolution fusion | flops 807599104 | bytes 4207616 | tf_op jit(solution)/shard_map/rnv,rkv->rnk/dot_general | solution.py:308
  205.5 1.6 fusion.28
  207.2 0.6 pad_maximum_fusion.1.x_ref
  207.8 11.2 %exchange.3 = f32[16,24,128]{2,1,0:T(8,128)} custom-call(f32[24,128]{1,0:T(8,128)} %pad_maximum_fusion.1.x_ref), custom_call_target="tpu_custom_call" | custom-call | tf_op jit(solution)/shard_map/exchange/pallas_call | solution.py:243
  219.0 1.0 reduce_sum.89
  220.1 0.3 fusion.40
  220.6 0.4 fusion.39
  221.0 0.4 fusion.38
  221.4 0.6 minimum_select_fusion.7
  222.1 0.3 fusion.37
  222.6 0.4 fusion.36
  223.1 0.4 fusion.35
  223.6 0.4 fusion.34
  224.1 0.4 fusion.33
  224.6 0.4 fusion.32
  225.1 0.4 fusion.31
  225.6 0.6 minimum_select_fusion
  226.2 0.6 slice_bitcast_fusion.3
  (51 shorter events, 2.0 us)
Async XLA Ops:
  176.9 5.7 %copy-start = (bf16[1024,1024]{1,0:T(8,128)(2,1)S(1)}, bf16[1024,1024]{1,0:T(8,128)(2,1)}, u32[]{:S(2)}) copy-start(bf16[1024,1024]{1,0:T(8,128)(2,1)} %param.11) | copy-start | bytes 6291460
  182.9 17.2 %copy-start.4 = (s32[1024]{0:T(1024)S(1)}, s32[1024]{0:T(1024)}, u32[]{:S(2)}) copy-start(s32[1024]{0:T(1024)} %param.13) | copy-start | bytes 12292
  183.0 17.3 %copy-start.6 = (s32[1024]{0:T(1024)S(1)}, s32[1024]{0:T(1024)}, u32[]{:S(2)}) copy-start(s32[1024]{0:T(1024)} %param.12) | copy-start | bytes 12292
  196.5 23.5 %copy-start.3 = (f32[8,128]{1,0:T(8,128)}, f32[8,128]{1,0:T(8,128)S(1)}, u32[]{:S(2)}) copy-start(f32[8,128]{1,0:T(8,128)S(1)} %get-tuple-element.17) | copy-start | bytes 12292
  205.4 16.0 %copy-start.1 = (s32[1024]{0:T(1024)S(1)}, s32[1024]{0:T(1024)}, u32[]{:S(2)}) copy-start(s32[1024]{0:T(1024)} %param.14) | copy-start | bytes 12292
  205.4 16.0 %copy-start.5 = (f32[1024]{0:T(1024)S(1)}, f32[1024]{0:T(1024)}, u32[]{:S(2)}) copy-start(f32[1024]{0:T(1024)} %param.15) | copy-start | bytes 12292
  222.0 4.8 %copy-start.2 = (f32[1024]{0:T(1024)}, f32[1024]{0:T(1024)S(1)}, u32[]{:S(2)}) copy-start(f32[1024]{0:T(1024)S(1)} %get-tuple-element.10) | copy-start | bytes 12292

commit v2 on v1

--- a/solution.py
+++ b/solution.py
@@ -25,51 +25,64 @@
     return scaled.astype(jnp.bfloat16)
 
 
+CYCLES = (
+    (0, 1, 3, 2, 6, 7, 5, 9, 11, 10, 14, 15, 13, 12, 8, 4),
+    (0, 1, 5, 4, 6, 10, 8, 9, 13, 12, 14, 15, 11, 7, 3, 2),
+    (0, 2, 6, 7, 3, 1, 5, 9, 13, 15, 11, 10, 14, 12, 8, 4),
+)
+LANE = 128
+
+
+def look_up(table, index):
+    value = jnp.int32(table[0])
+    for k in range(1, len(table)):
+        value = jnp.where(index == k, jnp.int32(table[k]), value)
+    return value
+
+
 def place_of(device, cycle, n):
     if n != 16:
         return device
-    z, y, x = device // 4, (device // 2) % 2, device % 2
-    corner = 2 * y + (x + y) % 2
-    step = (corner + z) % 4
-    return 4 * (z if cycle == 0 else corner) + step
+    order = CYCLES[cycle]
+    return look_up([order.index(k) for k in range(n)], device)
 
 
 def device_at(place, cycle, n):
     if n != 16:
         return place
-    major = place // 4
-    minor = (place % 4 + 4 - major) % 4
-    z, corner = (major, minor) if cycle == 0 else (minor, major)
-    y = corner // 2
-    x = (corner + y) % 2
-    return 4 * z + 2 * y + x
+    return look_up(CYCLES[cycle], place)
 
 
 def gather_dot_kernel(
-    n, parts, own_ref, head_ref, out_ref, held, head, own_sem, head_sem, send_sem, recv_sem
+    n, starts, widths, *refs
 ):
-    streams, rows, width = own_ref.shape
+    streams = len(widths)
+    owns, (head_ref, out_ref), helds = refs[:streams], refs[streams : streams + 2], refs[streams + 2 : -5]
+    head, own_sem, head_sem, send_sem, recv_sem = refs[-5:]
+    rows = owns[0].shape[0]
     group = max(1, min(n, CHUNK_ROWS // rows))
     chunks = n // group
     columns = out_ref.shape[2]
     me = lax.axis_index("vocab")
-    places = [place_of(me, cycle, n) for cycle in range(2)]
+    places = [place_of(me, cycle, n) for cycle in range(3)]
 
     def stream_kind(q):
-        lane = q // parts
-        return lane // 2, lane % 2
+        return q // 2, q % 2
 
     def partner(q, steps):
         cycle, backward = stream_kind(q)
         hop = (n - steps) if backward else steps
         return device_at(lax.rem(places[cycle] + hop, n), cycle, n)
 
-    own_copy = pltpu.make_async_copy(own_ref, held.at[0], own_sem)
-    own_copy.start()
+    own_copies = [
+        pltpu.make_async_copy(owns[q], helds[q].at[0], own_sem.at[q]) for q in range(streams)
+    ]
+    for own_copy in own_copies:
+        own_copy.start()
     head_copy = pltpu.make_async_copy(head_ref, head, head_sem)
     head_copy.start()
 
-    ways = [partner(q, 1) for q in range(0, streams, parts)]
+    ways = [partner(q, 1) for q in range(streams)]
     barrier = pltpu.get_barrier_semaphore()
     for target in ways:
         pl.semaphore_signal(barrier, inc=1, device_id={"vocab": target}, device_id_type=MESH)
@@ -77,35 +90,38 @@
 
     def copy_of(q, step):
         return pltpu.make_async_remote_copy(
-            src_ref=held.at[step, q],
-            dst_ref=held.at[step + 1, q],
+            src_ref=helds[q].at[step],
+            dst_ref=helds[q].at[step + 1],
             send_sem=send_sem.at[step, q],
             recv_sem=recv_sem.at[step, q],
-            device_id={"vocab": ways[q // parts]},
+            device_id={"vocab": ways[q]},
             device_id_type=MESH,
         )
 
     def multiply(chunk, q):
         first = chunk * group
+        cycle, backward = stream_kind(q)
+        owners = []
+        for g in range(group):
+            slot = first + g
+            place = places[cycle] + slot if backward else places[cycle] + n - slot
+            owners.append(device_at(lax.rem(place, n), cycle, n))
 
         def tile(index, _):
             at = pl.multiple_of(index * COLUMN_TILE, COLUMN_TILE)
-            block = jnp.concatenate([held[first + g, q] for g in range(group)], axis=0)
+            block = jnp.concatenate([helds[q][first + g] for g in range(group)], axis=0)
             part = jnp.dot(
-                block, head[q, :, pl.ds(at, COLUMN_TILE)], preferred_element_type=jnp.float32
+                block, head[starts[q] : starts[q] + widths[q], pl.ds(at, COLUMN_TILE)], preferred_element_type=jnp.float32
             )
             for g in range(group):
-                cycle, backward = stream_kind(q)
-                slot = first + g
-                place = places[cycle] + slot if backward else places[cycle] + n - slot
-                owner = device_at(lax.rem(place, n), cycle, n)
                 piece = part[g * rows : (g + 1) * rows]
-                out_ref[owner, :, pl.ds(at, COLUMN_TILE)] += piece
+                out_ref[owners[g], :, pl.ds(at, COLUMN_TILE)] += piece
             return 0
 
         lax.fori_loop(0, columns // COLUMN_TILE, tile, 0)
 
-    own_copy.wait()
+    for own_copy in own_copies:
+        own_copy.wait()
     for q in range(streams):
         copy_of(q, 0).start()
     head_copy.wait()
@@ -114,11 +130,11 @@
     return me, group, chunks, copy_of, multiply
 
 
-def gather_dot_body(n, parts, *refs):
-    streams = refs[0].shape[0]
-    _, group, chunks, copy_of, multiply = gather_dot_kernel(n, parts, *refs)
-    per_step = streams // group if group <= streams else 1
-    spread = streams // per_step
+def gather_dot_body(n, starts, widths, *refs):
+    streams = len(widths)
+    _, group, chunks, copy_of, multiply = gather_dot_kernel(n, starts, widths, *refs)
+    per_step = -(-streams // group)
+    spread = -(-streams // per_step)
 
     def run(chunk, turn):
         for k in range(per_step):
@@ -163,20 +179,22 @@
 
 def gather_dot(normed, lm_head, n):
     rows, depth = normed.shape
-    parts = 2 if n <= 16 else 1
-    streams = 4 * parts
-    width = depth // streams
+    streams = 2 * len(CYCLES)
+    tiles = depth // LANE
+    pairs = [tiles // 2 * k // len(CYCLES) for k in range(len(CYCLES) + 1)]
+    widths = [LANE * (pairs[q // 2 + 1] - pairs[q // 2]) for q in range(streams)]
+    starts = [sum(widths[:q]) for q in range(streams)]
     columns = lm_head.shape[1]
-    own = normed.reshape(rows, streams, width).transpose(1, 0, 2)
+    owns = [normed[:, at : at + width] for at, width in zip(starts, widths)]
     out = pl.pallas_call(
-        functools.partial(gather_dot_body, n, parts),
+        functools.partial(gather_dot_body, n, starts, widths),
         out_shape=jax.ShapeDtypeStruct((n, rows, columns), jnp.float32),
-        in_specs=[pl.BlockSpec(memory_space=pl.ANY)] * 2,
+        in_specs=[pl.BlockSpec(memory_space=pl.ANY)] * (streams + 1),
         out_specs=pl.BlockSpec(memory_space=pltpu.VMEM),
         scratch_shapes=[
-            pltpu.VMEM((n, streams, rows, width), jnp.bfloat16),
-            pltpu.VMEM((streams, width, columns), jnp.bfloat16),
-            pltpu.SemaphoreType.DMA,
+            *(pltpu.VMEM((n, rows, width), jnp.bfloat16) for width in widths),
+            pltpu.VMEM((depth, columns), jnp.bfloat16),
+            pltpu.SemaphoreType.DMA((streams,)),
             pltpu.SemaphoreType.DMA,
             pltpu.SemaphoreType.DMA((n - 1, streams)),
             pltpu.SemaphoreType.DMA((n - 1, streams)),
@@ -185,7 +203,7 @@
             collective_id=0, has_side_effects=True, vmem_limit_bytes=56 * 1024 * 1024
         ),
         name="gather_dot",
-    )(own, lm_head.reshape(streams, width, columns))
+    )(*owns, lm_head)
     return out.reshape(n * rows, columns)
 
 

time: 227 us -> 175 us (0.77)
  Pallas kernels: 193 us -> 140 us
    pallas_call x1, Pallas kernels: 172 us -> 118 us  [gather_dot(): pl.pallas_call(functools.partial(gather_dot_body, n, starts, widths), out...]
where the time goes in v2:
time: 175 us
  Pallas kernels  140 us (80%)
  other arithmetic  19.5 us (11%)
  matrix products  10 us (6%)
  local copies, waits for them, and re-layouts  4.09 us (2%)
    pallas_call x1, Pallas kernels, gather_dot(): pl.pallas_call(functools.partial(gather_dot_body, n, starts, widths), out...  118 us
    pallas_call x2, Pallas kernels, exchange(): pl.pallas_call(functools.partial(exchange_kernel, n), out_shape=jax.Shape...  21.8 us
    dot_general x1, matrix products, body(): jnp.einsum('rnv,rkv->rnk', logits.reshape(requests, NODES, vocab_dev), co...  5.01 us
    reduce_sum x1, other arithmetic, body(): jnp.sum(excess, axis=1)  3.81 us
    dot_general x10, matrix products, at_parent(): jnp.einsum('rkn,rn->rk', parent_hot, vector.reshape(requests, NODES), pre...  3.54 us

profile of v2, /device:TPU:0, one launch (start us, length us, event | category | flops | bytes accessed | tf_op | source)
XLA Modules:
  0.0 174.7 jit_solution(2612463058325111755)
XLA Ops:
  0.6 0.7 convert_element_type.16
  1.3 1.5 fusion.16
  2.8 1.5 fusion.18
  4.3 0.8 fusion.66
  5.1 0.7 fusion.65
  5.9 118.4 %gather_dot.1 = f32[16,64,1024]{2,1,0:T(8,128)} custom-call(bf16[64,1152]{1,0:T(8,128)(2,1)} %get-tuple-element.19.refs_0_, bf16[64,1152]{1,0:T(8,128)(2,1)} %get-tuple-element.18.refs_1_, bf16[64,1152]{1,0:T(8,128)(2,1)} %get-tuple-element.17.refs_2_, bf16[64,1152]{1,0:T(8,128)(2,1)} %get-tuple-element.16.refs_3_, ...), custom_call_target="tpu_custom_call" | custom-call | tf_op jit(solution)/shard_map/gather_dot/pallas_call | solution.py:189
  124.3 2.6 %reduce_max.45 = f32[16,64]{1,0:T(8,128)S(1)} reduce(f32[16,64,1024]{2,1,0:T(8,128)} %gather_dot.1, f32[]{:T(128)} %constant.6.clone.1), dimensions={2}, to_apply=%region_1.0 | reduce | flops 1047552 | bytes 4198404 | tf_op jit(solution)/shard_map/reduce_max | solution.py:303
  126.9 2.9 %exponential_reduce_fusion = f32[16,64]{1,0:T(8,128)S(1)} fusion(f32[16,64,1024]{2,1,0:T(8,128)} %gather_dot.1, f32[16,64]{1,0:T(8,128)S(1)} %reduce_max.45), kind=kLoop, calls=%fused_computation.11 | loop fusion | flops 2096128 | bytes 4202496 | tf_op jit(solution)/shard_map/reduce_sum | solution.py:308
  130.0 0.3 reduce_max.46
  130.4 0.9 fusion.1
  131.3 0.6 pad_maximum_fusion.x_ref
  131.9 11.3 %exchange.2 = f32[16,32,128]{2,1,0:T(8,128)} custom-call(f32[32,128]{1,0:T(8,128)} %pad_maximum_fusion.x_ref), custom_call_target="tpu_custom_call" | custom-call | tf_op jit(solution)/shard_map/exchange/pallas_call | solution.py:261
  143.2 0.9 bitcast_reduce_fusion
  144.1 1.0 fusion.52
  145.1 3.8 %fusion.5 = f32[1024]{0:T(1024)S(1)} fusion(bf16[1024,1024]{1,0:T(8,128)(2,1)S(1)} %copy-done, f32[16,64,1024]{2,1,0:T(8,128)} %gather_dot.1, f32[1024]{0:T(1024)S(1)} %bitcast.111, f32[1024]{0:T(1024)S(1)} %bitcast.109), kind=kLoop, calls=%fused_computation.7 | loop fusion | flops 6290432 | bytes 6303744 | tf_op jit(solution)/shard_map/reduce_sum | solution.py:340
  149.1 5.0 %fusion.25 = f32[16,64]{1,0:T(8,128)S(1)} fusion(f32[16,64,1024]{2,1,0:T(8,128)} %gather_dot.1, s32[16,64]{1,0:T(8,128)S(1)} %eq.83, pred[16,64]{1,0:T(8,128)(4,1)S(1)} %and.16, s32[16,64]{1,0:T(8,128)S(1)} %eq.79), kind=kOutput, calls=%fused_computation.26 | convolution fusion | flops 807599104 | bytes 4207616 | tf_op jit(solution)/shard_map/rnv,rkv->rnk/dot_general | solution.py:326
  154.2 1.5 fusion.28
  155.8 0.6 pad_maximum_fusion.1.x_ref
  156.4 10.6 %exchange.3 = f32[16,24,128]{2,1,0:T(8,128)} custom-call(f32[24,128]{1,0:T(8,128)} %pad_maximum_fusion.1.x_ref), custom_call_target="tpu_custom_call" | custom-call | tf_op jit(solution)/shard_map/exchange/pallas_call | solution.py:261
  166.9 1.0 reduce_sum.89
  168.0 0.3 fusion.40
  168.5 0.4 fusion.39
  168.9 0.4 fusion.38
  169.3 0.6 minimum_select_fusion.7
  170.5 0.4 fusion.36
  171.0 0.4 fusion.35
  171.5 0.4 fusion.34
  172.0 0.4 fusion.33
  172.6 0.4 fusion.32
  173.1 0.4 fusion.31
  173.5 0.6 minimum_select_fusion
  174.1 0.6 slice_bitcast_fusion.3
  (52 shorter events, 2.3 us)
Async XLA Ops:
  124.3 5.7 %copy-start = (bf16[1024,1024]{1,0:T(8,128)(2,1)S(1)}, bf16[1024,1024]{1,0:T(8,128)(2,1)}, u32[]{:S(2)}) copy-start(bf16[1024,1024]{1,0:T(8,128)(2,1)} %param.11) | copy-start | bytes 6291460
  130.3 18.5 %copy-start.4 = (s32[1024]{0:T(1024)S(1)}, s32[1024]{0:T(1024)}, u32[]{:S(2)}) copy-start(s32[1024]{0:T(1024)} %param.13) | copy-start | bytes 12292
  130.4 18.6 %copy-start.6 = (s32[1024]{0:T(1024)S(1)}, s32[1024]{0:T(1024)}, u32[]{:S(2)}) copy-start(s32[1024]{0:T(1024)} %param.12) | copy-start | bytes 12292
  145.0 22.9 %copy-start.3 = (f32[8,128]{1,0:T(8,128)}, f32[8,128]{1,0:T(8,128)S(1)}, u32[]{:S(2)}) copy-start(f32[8,128]{1,0:T(8,128)S(1)} %get-tuple-element.23) | copy-start | bytes 12292
  154.1 15.2 %copy-start.1 = (s32[1024]{0:T(1024)S(1)}, s32[1024]{0:T(1024)}, u32[]{:S(2)}) copy-start(s32[1024]{0:T(1024)} %param.14) | copy-start | bytes 12292
  154.1 15.2 %copy-start.5 = (f32[1024]{0:T(1024)S(1)}, f32[1024]{0:T(1024)}, u32[]{:S(2)}) copy-start(f32[1024]{0:T(1024)} %param.15) | copy-start | bytes 12292
  169.9 4.8 %copy-start.2 = (f32[1024]{0:T(1024)}, f32[1024]{0:T(1024)S(1)}, u32[]{:S(2)}) copy-start(f32[1024]{0:T(1024)S(1)} %get-tuple-element.10) | copy-start | bytes 12292
